TPU v7x, 128 devices: a whole 4x4x4 slice. The times are simulated.
128 devices in a mesh: band: 64 (over y, z_lo, x, core), ga: 2 (over z_hi).
Axes of the slice: x: 4, y: 4, z: 4 (z_hi: 2, z_lo: 2; z = z_hi * 2 + z_lo), core: 2. Of those that a mesh axis runs over, the one named last changes fastest.
Arguments:
- matrix_elements: float32 [2, 16384, 12288], P(None, 'band', 'ga'), may hold values from -16 to 16
- band_index: int32 [16384], P('band'), may hold values from 0 to 1048575
- occupied: int32 [1], replicated, may hold values from 262144 to 786432
- band_weight: float32 [16384], P('band'), may hold values from 0.3 to 3
- coulomb: float32 [12288], replicated, may hold values from 0.2 to 5
Outputs:
- sigma: float32 [12288, 2, 512], P(('ga', 'band'))
All inputs are finite; a program needn't handle non-finite values.
Results may differ from a plain program's by a relative error of at most 0.00018.
Values sent between devices are 32-bit elements; how exact they have to be, the bound alone decides.
A program may use at most 192 MiB of HBM per device.

v0:
```python
import math
import jax
import jax.numpy as jnp
from jax import lax
from jax.sharding import Mesh
from jax.sharding import PartitionSpec as P

COLS = 512
BAND = ("band_0", "band_1", "band_2", "band_3")
GA_BAND = ("ga", "band_0", "band_1", "band_2", "band_3")


def spread(x, axis, root):
    mine = lax.axis_index(axis) == root
    return lax.psum(jnp.where(mine, x, jnp.zeros_like(x)), axis)


def in_blocks(x, dim, length):
    before, after = (x.shape[:dim], x.shape[dim + 1 :])
    return jnp.moveaxis(x.reshape(*before, length, -1, *after), dim, 0)


def sum_by_chip(x, chips, core, dim):
    sizes = (lax.axis_size(chips), lax.axis_size(core))
    blocks = in_blocks(x, dim, sizes[0] * sizes[1])
    inside = blocks.shape[1:]
    blocks = blocks.reshape(*sizes, *inside).swapaxes(0, 1).reshape(-1, *inside)
    blocks = lax.psum_scatter(blocks, core, scatter_dimension=0, tiled=True)
    return lax.psum_scatter(blocks, chips, scatter_dimension=0, tiled=True)[0]


def sent_and_summed(x, axis, dim):
    blocks = in_blocks(x, dim, lax.axis_size(axis))
    arrived = lax.all_to_all(blocks, axis, split_axis=0, concat_axis=0, tiled=True)
    return arrived.sum(axis=0)


def one_axis_at_a_time(x, axes):
    for axis in axes:
        x = lax.psum(x, axis)
    return x


def contract(left, right):
    return lax.dot_general(
        left,
        right,
        (((0,), (0,)), ((), ())),
        precision=lax.Precision.HIGHEST,
        preferred_element_type=jnp.float32,
    )


def right_side(slab):
    return jnp.concatenate(
        [jnp.concatenate([slab[0], slab[1]], 1), jnp.concatenate([slab[1], -slab[0]], 1)], 0
    )


def defects(coef, block):
    square = 2.0 - block[0] * block[0] - block[1] * block[1]
    return jnp.dot(
        coef, square, precision=lax.Precision.HIGHEST, preferred_element_type=jnp.float32
    )


def body(matrix_elements, band_index, occupied, band_weight, coulomb):
    bands_dev = matrix_elements.shape[1]
    half = matrix_elements.shape[2]
    n_band = lax.axis_size(BAND)
    rows_dev = half // n_band
    factor = 1.0 / math.sqrt(bands_dev * n_band)
    occ = (band_index < occupied[0]).astype(jnp.float32)
    coef = (0.5 - occ) * band_weight
    slab = spread(matrix_elements[:, :, :COLS], "ga", 0)
    band_pos = lax.axis_index(BAND)
    ga_pos = lax.axis_index("ga")
    left = jnp.concatenate(
        [coef[:, None] * matrix_elements[0], coef[:, None] * matrix_elements[1]], 0
    )
    right = right_side(slab)
    sums = sum_by_chip(contract(left, right), ("band_0", "band_1", "band_2"), "band_3", 0)
    defect_full = defects(coef, matrix_elements)
    defect_slab = defects(coef, slab)
    row_def = sent_and_summed(defect_full, BAND, 0)
    col_def = one_axis_at_a_time(defect_slab, BAND)
    sums = sums * factor
    row_def = row_def * factor
    col_def = col_def * factor
    row_coul = lax.dynamic_slice_in_dim(coulomb, ga_pos * half + band_pos * rows_dev, rows_dev, 0)
    weight = jnp.sqrt(row_coul[:, None] * coulomb[None, :COLS])
    part_re = weight * (sums[:, :COLS] + 0.5 * (row_def[:, None] + col_def[None, :]))
    part_im = weight * sums[:, COLS:]
    return jnp.stack([part_re, part_im], 1)


def solution(mesh):
    finer = Mesh(
        mesh.devices.reshape(4, 2, 4, 2, mesh.shape["ga"]),
        ("band_0", "band_1", "band_2", "band_3", "ga"),
    )
    in_specs = (P(None, BAND, "ga"), P(BAND), P(), P(BAND), P())
    out_specs = P(GA_BAND, None, None)
    return jax.shard_map(body, mesh=finer, in_specs=in_specs, out_specs=out_specs, check_vma=False)
```

profile of v0, /device:TPU:64, one launch (start us, length us, event | category | flops | bytes accessed | tf_op | source)
XLA Modules:
  0.0 369.5 jit_solution(3057454762529198475)
XLA Ops:
  6.5 2.4 slice_select_fusion
  9.0 10.6 %fusion.27 = (f32[1,256,6144]{2,1,0:T(8,128)}, f32[1,256,6144]{2,1,0:T(8,128)}) fusion(f32[2,256,6144]{2,1,0:T(8,128)} %param.5), kind=kLoop, calls=%fused_computation.43 | loop fusion | bytes 25165824 | tf_op jit(solution)/shard_map/slice | solution.py:79
  20.3 6.7 %copy.17 = f32[1,256,6144]{1,2,0:T(8,128)} copy(f32[1,256,6144]{2,1,0:T(8,128)} %get-tuple-element.5) | data formatting | bytes 12582912
  26.9 6.7 %copy.18 = f32[1,256,6144]{1,2,0:T(8,128)} copy(f32[1,256,6144]{2,1,0:T(8,128)} %get-tuple-element.6) | data formatting | bytes 12582912
  33.6 11.6 %fusion.4 = (f32[256,6144]{0,1:T(8,128)}, f32[256,6144]{0,1:T(8,128)}, f32[256,6144]{0,1:T(8,128)}) fusion(f32[1,256,6144]{1,2,0:T(8,128)} %copy.18, f32[1,256,6144]{1,2,0:T(8,128)} %copy.17, f32[256]{0:T(256)S(1)} %fusion.23), kind=kLoop, calls=%fused_computation.6 | loop fusion | flops 9437184 | bytes 31458304 | tf_op jit(solution)/shard_map/sub | solution.py:61
  45.2 11.5 %all-reduce.2.cloned.1.call-done = f32[2,256,512]{2,1,0:T(8,128)} async-done(((f32[2,256,512]{2,1,0:T(8,128)}), f32[2,256,512]{2,1,0:T(8,128)}) %all-reduce.2.cloned.1.call-update) | async-done | bytes 1048592 | tf_op jit(solution)/shard_map/psum | solution.py:15
  56.7 1.1 fusion.26
  57.8 1.3 slice_bitcast_fusion.1
  59.1 45.8 %fusion = f32[6144,1024]{1,0:T(8,128)} fusion(f32[256,6144]{0,1:T(8,128)} %get-tuple-element.9, f32[256,6144]{0,1:T(8,128)} %get-tuple-element.8, f32[256,512]{1,0:T(8,128)S(1)} %fusion.26, f32[256,512]{1,0:T(8,128)S(1)} %get-tuple-element.11, f32[256,512]{1,0:T(8,128)S(1)} %get-tuple-element.10), kind=kOutput, calls=%fused_computation | convolution fusion | flops 38659424256 | bytes 39321600 | tf_op jit(solution)/shard_map/dot_general | solution.py:45
  104.9 17.7 %copy.14 = f32[2,32,96,1024]{3,2,1,0:T(8,128)} copy(f32[2,32,96,1024]{3,2,0,1:T(8,128)} %bitcast.49) | data formatting | bytes 50331648 | tf_op jit(solution)/shard_map/transpose | solution.py:27
  122.6 41.9 %reduce-scatter.3.cloned.1.call-done = f32[32,96,1024]{2,1,0:T(8,128)} async-done(((f32[64,96,1024]{2,1,0:T(8,128)}), f32[32,96,1024]{2,1,0:T(8,128)}) %reduce-scatter.3.cloned.1.call-update) | async-done | bytes 12582928 | tf_op jit(solution)/shard_map/reduce_scatter | solution.py:28
  164.6 14.4 %convolution_bitcast_fusion = f32[64,1,96]{2,1,0:T(1,128)} fusion(f32[256,1,1]{0,1,2:T(1,128)S(1)} %bitcast.52, f32[64,96,256]{2,1,0:T(8,128)} %bitcast.51), kind=kOutput, calls=%fused_computation.17 | convolution fusion | flops 18874368 | bytes 6317056 | tf_op jit(solution)/shard_map/dot_general | solution.py:62
  179.0 8.4 %all-to-all-start = ((f32[64,1,96]{2,1,0:T(1,128)}), f32[64,1,96]{2,1,0:T(1,128)S(1)}, u32[]{:S(2)}, u32[]{:S(2)}) async-start(f32[64,1,96]{2,1,0:T(1,128)} %convolution_bitcast_fusion), calls=%async_computation.2 | async-start | bytes 65536 | tf_op jit(solution)/shard_map/all_to_all | solution.py:34
  187.5 8.0 %all-to-all-done = f32[64,1,96]{2,1,0:T(1,128)S(1)} async-done(((f32[64,1,96]{2,1,0:T(1,128)}), f32[64,1,96]{2,1,0:T(1,128)S(1)}, u32[]{:S(2)}, u32[]{:S(2)}) %all-to-all-start) | async-done | bytes 24608 | tf_op jit(solution)/shard_map/all_to_all | solution.py:34
  195.6 0.1 reduce_sum.9
  195.6 0.4 fusion.13
  196.1 8.6 %psum.36 = f32[512]{0:T(512)S(1)} all-reduce(f32[512]{0:T(512)S(1)} %bitcast.54), channel_id=1, replica_groups=mesh['band_0'=4,'band_1'=2,'band_2'=4,'band_3'=2,'ga'=2] {'band_0'}, use_global_device_ids=true, to_apply=%region_4.5 | all-reduce | flops 512 | bytes 4096 | tf_op jit(solution)/shard_map/psum | solution.py:40
  204.7 5.3 %psum.37 = f32[512]{0:T(512)S(1)} all-reduce(f32[512]{0:T(512)S(1)} %psum.36), channel_id=1, replica_groups=mesh['band_0'=4,'band_1'=2,'band_2'=4,'band_3'=2,'ga'=2] {'band_1'}, use_global_device_ids=true, to_apply=%region_5.6 | all-reduce | flops 512 | bytes 4096 | tf_op jit(solution)/shard_map/psum | solution.py:40
  210.0 11.4 %psum.38 = f32[512]{0:T(512)S(1)} all-reduce(f32[512]{0:T(512)S(1)} %psum.37), channel_id=1, replica_groups=mesh['band_0'=4,'band_1'=2,'band_2'=4,'band_3'=2,'ga'=2] {'band_2'}, use_global_device_ids=true, to_apply=%region_6.7 | all-reduce | flops 512 | bytes 4096 | tf_op jit(solution)/shard_map/psum | solution.py:40
  221.4 2.5 psum.39
  223.8 136.9 %reduce-scatter.5.cloned.1.call-done = f32[1,96,1024]{2,1,0:T(8,128)} async-done(((f32[32,96,1024]{2,1,0:T(8,128)}), f32[1,96,1024]{2,1,0:T(8,128)}) %reduce-scatter.5.cloned.1.call-update) | async-done | bytes 393232 | tf_op jit(solution)/shard_map/reduce_scatter | solution.py:29
  360.7 1.0 multiply_bitcast_fusion
  361.7 0.2 fusion.21
  361.9 1.1 copy.15
  (21 shorter events, 0.3 us)
Async XLA Ops:
  6.5 50.2 %all-reduce.2.cloned.1.call-start = ((), (), s32[]{:S(2)}) async-start(), calls=%async_computation.3 | async-start | bytes 2097152 | tf_op jit(solution)/shard_map/psum | solution.py:15
  8.9 155.6 %reduce-scatter.3.cloned.1.call-start = ((), (), s32[]{:S(2)}) async-start(), calls=%async_computation.4 | async-start | bytes 37748736 | tf_op jit(solution)/shard_map/reduce_scatter | solution.py:28
  26.9 6.7 %copy-start.2 = (f32[256]{0:T(256)S(1)}, f32[256]{0:T(256)}, u32[]{:S(2)}) copy-start(f32[256]{0:T(256)} %param.8) | copy-start | bytes 3076
  26.9 6.7 %copy-start.3 = (s32[256]{0:T(256)S(1)}, s32[256]{0:T(256)}, u32[]{:S(2)}) copy-start(s32[256]{0:T(256)} %param.6) | copy-start | bytes 3076
  122.6 238.1 %reduce-scatter.5.cloned.1.call-start = ((), (), s32[]{:S(2)}) async-start(), calls=%async_computation.5 | async-start | bytes 12976128 | tf_op jit(solution)/shard_map/reduce_scatter | solution.py:29
  164.5 22.9 %copy-start.1 = (f32[12288]{0:T(1024)S(1)}, f32[12288]{0:T(1024)}, u32[]{:S(2)}) copy-start(f32[12288]{0:T(1024)} %param.9) | copy-start | bytes 147460
  164.5 31.1 %copy-start = (f32[2,256,512]{2,1,0:T(8,128)S(1)}, f32[2,256,512]{2,1,0:T(8,128)}, u32[]{:S(2)}) copy-start(f32[2,256,512]{2,1,0:T(8,128)} %all-reduce.2.cloned.1.call-done) | copy-start | bytes 3145732
  164.6 197.2 %slice-start = ((f32[12288]{0:T(1024)}), f32[512]{0:T(512)S(1)}, s32[]{:S(2)}) async-start(f32[12288]{0:T(1024)} %param.9), calls=%async_computation.6 | async-start | bytes 4096 | tf_op jit(solution)/shard_map/slice | solution.py:91
  179.0 16.6 %all-to-all-start = ((f32[64,1,96]{2,1,0:T(1,128)}), f32[64,1,96]{2,1,0:T(1,128)S(1)}, u32[]{:S(2)}, u32[]{:S(2)}) async-start(f32[64,1,96]{2,1,0:T(1,128)} %convolution_bitcast_fusion), calls=%async_computation.2 | async-start | bytes 65536 | tf_op jit(solution)/shard_map/all_to_all | solution.py:34
Sparse Core Ops, SparseCore 0:
  9.8 46.9 all-reduce.1
  122.7 41.7 reduce-scatter.2
  166.9 193.7 reduce-scatter.4
where the time goes:
time: 370 us
  waiting for transfers between devices  198 us (54%)
  matrix products  60.6 us (16%)
  local copies, waits for them, and re-layouts  44.1 us (12%)
  blocking collectives  27.8 us (8%)
  other arithmetic  16.3 us (4%)
  between operations  13.9 us (4%)
  starting transfers between devices  8.52 us (2%)
    reduce_scatter x1, waiting for transfers between devices, sum_by_chip(): return lax.psum_scatter(blocks, chips, scatter_dimension=0, tiled=True)[0]  137 us
    dot_general x1, matrix products, contract(): lax.dot_general(left, right, (((0,), (0,)), ((), ())), precision=lax.Prec...  45.8 us
    reduce_scatter x1, waiting for transfers between devices, sum_by_chip(): blocks = lax.psum_scatter(blocks, core, scatter_dimension=0, tiled=True)  41.9 us
    psum x4, blocking collectives, one_axis_at_a_time(): x = lax.psum(x, axis)  27.8 us
    transpose x1, local copies, waits for them, and re-layouts, sum_by_chip(): blocks = blocks.reshape(*sizes, *inside).swapaxes(0, 1).reshape(-1, *inside)  17.7 us
    dot_general x2, matrix products, defects(): jnp.dot(coef, square, precision=lax.Precision.HIGHEST, preferred_element_...  14.8 us
    unnamed x10, local copies, waits for them, and re-layouts  13.4 us
    sub x1, other arithmetic, defects(): square = 2.0 - block[0] * block[0] - block[1] * block[1]  11.6 us
  transfers between devices with their start and end apart: 4, of which 4 were waited for; matrix products, arithmetic and copies ran while one was open for 14% of the time, Pallas kernels for 0%

commit v1 on v0

--- a/solution.py
+++ b/solution.py
@@ -12,7 +12,7 @@
 
 def spread(x, axis, root):
     mine = lax.axis_index(axis) == root
-    return lax.psum(jnp.where(mine, x, jnp.zeros_like(x)), axis)
+    return jnp.sum(lax.all_gather(jnp.where(mine, x, jnp.zeros_like(x)), axis), axis=0)
 
 
 def in_blocks(x, dim, length):

time: 370 us -> 358 us (0.968)
  waiting for transfers between devices: 198 us -> 188 us
    psum x1 -> x0, waiting for transfers between devices: 11.5 us -> none  [spread(): return lax.psum(jnp.where(mine, x, jnp.zeros_like(x)), axis)]
    unnamed x10 -> x8, local copies, waits for them, and re-layouts: 13.4 us -> 13.5 us
  transfers between devices with their start and end apart: 4 -> 4, of which waited for: 4 -> 3; matrix products, arithmetic and copies ran while one was open for 14% -> 14% of each run, Pallas kernels for 0% -> 0%
where the time goes in v1:
time: 358 us; the launch traced here: 357 us
  waiting for transfers between devices  188 us (53%)
  matrix products  60.5 us (17%)
  local copies, waits for them, and re-layouts  43.2 us (12%)
  blocking collectives  25.8 us (7%)
  other arithmetic  16.9 us (5%)
  between operations  13.9 us (4%)
  starting transfers between devices  8.5 us (2%)
    reduce_scatter x1, waiting for transfers between devices, sum_by_chip(): return lax.psum_scatter(blocks, chips, scatter_dimension=0, tiled=True)[0]  138 us
    dot_general x1, matrix products, contract(): lax.dot_general(left, right, (((0,), (0,)), ((), ())), precision=lax.Prec...  45.8 us
    reduce_scatter x1, waiting for transfers between devices, sum_by_chip(): blocks = lax.psum_scatter(blocks, core, scatter_dimension=0, tiled=True)  41.6 us
    psum x4, blocking collectives, one_axis_at_a_time(): x = lax.psum(x, axis)  25.8 us
    transpose x1, local copies, waits for them, and re-layouts, sum_by_chip(): blocks = blocks.reshape(*sizes, *inside).swapaxes(0, 1).reshape(-1, *inside)  17.7 us
    dot_general x2, matrix products, defects(): jnp.dot(coef, square, precision=lax.Precision.HIGHEST, preferred_element_...  14.7 us
    unnamed x8, local copies, waits for them, and re-layouts  13.5 us
    sub x1, other arithmetic, defects(): square = 2.0 - block[0] * block[0] - block[1] * block[1]  11.4 us
  transfers between devices with their start and end apart: 4, of which 3 were waited for; matrix products, arithmetic and copies ran while one was open for 14% of the time, Pallas kernels for 0%

profile of v1, /device:TPU:64, one launch (start us, length us, event | category | flops | bytes accessed | tf_op | source)
XLA Modules:
  0.0 356.7 jit_solution(13291660949707123019)
XLA Ops:
  6.5 2.3 slice_select_fusion
  8.9 10.8 %fusion.27 = (f32[1,256,6144]{2,1,0:T(8,128)}, f32[1,256,6144]{2,1,0:T(8,128)}) fusion(f32[2,256,6144]{2,1,0:T(8,128)} %param.5), kind=kLoop, calls=%fused_computation.43 | loop fusion | bytes 25165824 | tf_op jit(solution)/shard_map/slice | solution.py:79
  20.3 6.9 %copy.17 = f32[1,256,6144]{1,2,0:T(8,128)} copy(f32[1,256,6144]{2,1,0:T(8,128)} %get-tuple-element.5) | data formatting | bytes 12582912
  27.2 6.7 %copy.18 = f32[1,256,6144]{1,2,0:T(8,128)} copy(f32[1,256,6144]{2,1,0:T(8,128)} %get-tuple-element.6) | data formatting | bytes 12582912
  33.9 11.4 %fusion.4 = (f32[256,6144]{0,1:T(8,128)}, f32[256,6144]{0,1:T(8,128)}, f32[256,6144]{0,1:T(8,128)}) fusion(f32[1,256,6144]{1,2,0:T(8,128)} %copy.18, f32[1,256,6144]{1,2,0:T(8,128)} %copy.17, f32[256]{0:T(256)S(1)} %fusion.23), kind=kLoop, calls=%fused_computation.6 | loop fusion | flops 9437184 | bytes 31458304 | tf_op jit(solution)/shard_map/sub | solution.py:61
  45.3 1.9 reduce_sum.18
  47.2 0.1 slice_bitcast_fusion.1
  47.3 45.8 %fusion = f32[6144,1024]{1,0:T(8,128)} fusion(f32[256,6144]{0,1:T(8,128)} %get-tuple-element.9, f32[256,6144]{0,1:T(8,128)} %get-tuple-element.8, f32[256,512]{1,0:T(8,128)S(1)} %fusion.26, f32[256,512]{1,0:T(8,128)S(1)} %get-tuple-element.11, f32[256,512]{1,0:T(8,128)S(1)} %get-tuple-element.10), kind=kOutput, calls=%fused_computation | convolution fusion | flops 38659424256 | bytes 39321600 | tf_op jit(solution)/shard_map/dot_general | solution.py:45
  93.1 17.7 %copy.14 = f32[2,32,96,1024]{3,2,1,0:T(8,128)} copy(f32[2,32,96,1024]{3,2,0,1:T(8,128)} %bitcast.50) | data formatting | bytes 50331648 | tf_op jit(solution)/shard_map/transpose | solution.py:27
  110.8 41.6 %reduce-scatter.3.cloned.1.call-done = f32[32,96,1024]{2,1,0:T(8,128)} async-done(((f32[64,96,1024]{2,1,0:T(8,128)}), f32[32,96,1024]{2,1,0:T(8,128)}) %reduce-scatter.3.cloned.1.call-update) | async-done | bytes 12582928 | tf_op jit(solution)/shard_map/reduce_scatter | solution.py:28
  152.5 14.3 %convolution_bitcast_fusion = f32[64,1,96]{2,1,0:T(1,128)} fusion(f32[256,1,1]{0,1,2:T(1,128)S(1)} %bitcast.54, f32[64,96,256]{2,1,0:T(8,128)} %bitcast.52), kind=kOutput, calls=%fused_computation.17 | convolution fusion | flops 18874368 | bytes 6317056 | tf_op jit(solution)/shard_map/dot_general | solution.py:62
  166.8 8.4 %all-to-all-start = ((f32[64,1,96]{2,1,0:T(1,128)}), f32[64,1,96]{2,1,0:T(1,128)S(1)}, u32[]{:S(2)}, u32[]{:S(2)}) async-start(f32[64,1,96]{2,1,0:T(1,128)} %convolution_bitcast_fusion), calls=%async_computation.2 | async-start | bytes 65536 | tf_op jit(solution)/shard_map/all_to_all | solution.py:34
  175.2 0.1 dynamic_slice.3
  175.3 8.0 %all-to-all-done = f32[64,1,96]{2,1,0:T(1,128)S(1)} async-done(((f32[64,1,96]{2,1,0:T(1,128)}), f32[64,1,96]{2,1,0:T(1,128)S(1)}, u32[]{:S(2)}, u32[]{:S(2)}) %all-to-all-start) | async-done | bytes 24608 | tf_op jit(solution)/shard_map/all_to_all | solution.py:34
  183.4 0.1 reduce_sum.19
  183.5 0.4 fusion.13
  183.9 8.6 %psum.28 = f32[512]{0:T(512)S(1)} all-reduce(f32[512]{0:T(512)S(1)} %bitcast.56), channel_id=1, replica_groups=mesh['band_0'=4,'band_1'=2,'band_2'=4,'band_3'=2,'ga'=2] {'band_0'}, use_global_device_ids=true, to_apply=%region_4.5 | all-reduce | flops 512 | bytes 4096 | tf_op jit(solution)/shard_map/psum | solution.py:40
  192.5 5.3 %psum.29 = f32[512]{0:T(512)S(1)} all-reduce(f32[512]{0:T(512)S(1)} %psum.28), channel_id=1, replica_groups=mesh['band_0'=4,'band_1'=2,'band_2'=4,'band_3'=2,'ga'=2] {'band_1'}, use_global_device_ids=true, to_apply=%region_5.6 | all-reduce | flops 512 | bytes 4096 | tf_op jit(solution)/shard_map/psum | solution.py:40
  197.8 9.5 %psum.30 = f32[512]{0:T(512)S(1)} all-reduce(f32[512]{0:T(512)S(1)} %psum.29), channel_id=1, replica_groups=mesh['band_0'=4,'band_1'=2,'band_2'=4,'band_3'=2,'ga'=2] {'band_2'}, use_global_device_ids=true, to_apply=%region_6.7 | all-reduce | flops 512 | bytes 4096 | tf_op jit(solution)/shard_map/psum | solution.py:40
  207.3 2.5 psum.31
  209.7 138.2 %reduce-scatter.5.cloned.1.call-done = f32[1,96,1024]{2,1,0:T(8,128)} async-done(((f32[32,96,1024]{2,1,0:T(8,128)}), f32[1,96,1024]{2,1,0:T(8,128)}) %reduce-scatter.5.cloned.1.call-update) | async-done | bytes 393232 | tf_op jit(solution)/shard_map/reduce_scatter | solution.py:29
  347.9 1.0 multiply_bitcast_fusion
  348.9 0.2 fusion.21
  349.1 1.1 copy.15
  (20 shorter events, 0.2 us)
Async XLA Ops:
  6.5 38.7 %all-gather.3.cloned.1.call-start = ((), (), s32[]{:S(2)}) async-start(), calls=%async_computation.5 | async-start | bytes 3145728 | tf_op jit(solution)/shard_map/all_gather | solution.py:15
  8.9 143.6 %reduce-scatter.3.cloned.1.call-start = ((), (), s32[]{:S(2)}) async-start(), calls=%async_computation.3 | async-start | bytes 37748736 | tf_op jit(solution)/shard_map/reduce_scatter | solution.py:28
  27.2 6.7 %copy-start.1 = (f32[256]{0:T(256)S(1)}, f32[256]{0:T(256)}, u32[]{:S(2)}) copy-start(f32[256]{0:T(256)} %param.8) | copy-start | bytes 3076
  27.2 6.7 %copy-start.2 = (s32[256]{0:T(256)S(1)}, s32[256]{0:T(256)}, u32[]{:S(2)}) copy-start(s32[256]{0:T(256)} %param.6) | copy-start | bytes 3076
  110.8 237.1 %reduce-scatter.5.cloned.1.call-start = ((), (), s32[]{:S(2)}) async-start(), calls=%async_computation.4 | async-start | bytes 12976128 | tf_op jit(solution)/shard_map/reduce_scatter | solution.py:29
  152.5 22.8 %copy-start = (f32[12288]{0:T(1024)S(1)}, f32[12288]{0:T(1024)}, u32[]{:S(2)}) copy-start(f32[12288]{0:T(1024)} %param.9) | copy-start | bytes 147460
  152.5 196.4 %slice-start = ((f32[12288]{0:T(1024)}), f32[512]{0:T(512)S(1)}, s32[]{:S(2)}) async-start(f32[12288]{0:T(1024)} %param.9), calls=%async_computation.6 | async-start | bytes 4096 | tf_op jit(solution)/shard_map/slice | solution.py:91
  166.8 16.6 %all-to-all-start = ((f32[64,1,96]{2,1,0:T(1,128)}), f32[64,1,96]{2,1,0:T(1,128)S(1)}, u32[]{:S(2)}, u32[]{:S(2)}) async-start(f32[64,1,96]{2,1,0:T(1,128)} %convolution_bitcast_fusion), calls=%async_computation.2 | async-start | bytes 65536 | tf_op jit(solution)/shard_map/all_to_all | solution.py:34
Sparse Core Ops, SparseCore 0:
  9.0 35.9 all-gather.2
  110.9 41.4 reduce-scatter.2
  154.9 192.9 reduce-scatter.4
